TPU v7x, 16 devices: a whole 2x2x2 slice. The times are simulated.
16 devices in a mesh: dp: 2 (over z), cp: 8 (over y, x, core).
Axes of the slice: x: 2, y: 2, z: 2, core: 2. Of those that a mesh axis runs over, the one named last changes fastest.
Arguments:
- x: bfloat16 [32, 7168], P('dp'), parts along dimension 0
- w_dq: bfloat16 [7168, 1536], replicated
- g_q: float32 [1536], replicated
- w_uq: bfloat16 [1536, 24576], replicated
- w_dkv: bfloat16 [7168, 576], replicated
- g_kv: float32 [512], replicated
- w_uk: bfloat16 [512, 128, 128], replicated
- w_uv: bfloat16 [512, 128, 128], replicated
- w_o: bfloat16 [16384, 7168], replicated
- cache_c: bfloat16 [32, 32768, 512], P('dp', 'cp'), parts along dimension 0
- cache_kr: bfloat16 [32, 32768, 64], P('dp', 'cp'), parts along dimension 0
- ctx_len: int32 [32], P('dp'), parts along dimension 0
Outputs:
- output 1: bfloat16 [32, 7168], P('dp'), parts along dimension 0
- output 2: bfloat16 [32, 512], P('dp'), parts along dimension 0
- output 3: bfloat16 [32, 64], P('dp'), parts along dimension 0
There are 2 independent parts. A program takes and returns all parts, laid end to end along the dimension named above; an argument that names none is the same for every part.
All inputs are finite; a program needn't handle non-finite values.
Results may differ from a plain program's by a relative error of at most 0.0063435.
Values sent between devices are 32-bit elements.
A program may use at most 1.75 GiB of HBM per device.

v0:
```python
import functools

import jax
import jax.numpy as jnp
from jax import lax
from jax.experimental import pallas as pl
from jax.experimental.pallas import tpu as pltpu
from jax.sharding import PartitionSpec as P

NORM_EPS = 1e-6
ROPE_THETA = 10000.0
MASKED = -1e30
FLOOR = -1e29
LOG2E = 1.4426950408889634


def exchange(src, dst, send_sem, recv_sem, peer):
    return pltpu.make_async_remote_copy(
        src_ref=src, dst_ref=dst, send_sem=send_sem, recv_sem=recv_sem,
        device_id={'cp': peer}, device_id_type=pl.DeviceIdType.MESH)


def merge(parts, latent):
    tops = [p[:, latent:latent + 1] for p in parts]
    top = functools.reduce(jnp.maximum, tops)
    acc, mass = None, None
    for p, t in zip(parts, tops):
        f = jnp.exp(t - top)
        a, w = p[:, :latent] * f, p[:, latent + 64:latent + 65] * f
        acc = a if acc is None else acc + a
        mass = w if mass is None else mass + w
    return acc, top, mass


def stats(top, mass):
    lane = lax.broadcasted_iota(jnp.int32, (top.shape[0], 128), 1)
    return jnp.where(lane < 64, top, mass)


def decode_body(
        dims, ctx_ref, x_ref, gq_ref, gkv_ref, tab_ref, dq_hbm, uq_hbm, dkv_hbm, uk_hbm, c_hbm, kr_hbm, uv_hbm, wo_hbm, out_ref,
        wo_buf, uk_buf, s_ref, turn_ref, cq_ref, kv_ref, norm_ref, q_ref, cn_ref, kn_ref,
        c_buf, kr_buf, acc_buf, recv_a, comb, recv_b, own_b, olat_ref, o_ref,
        po_ref, pair_ref, sum_ref, quart_ref, fin_ref, xo_ref,
        dq_sem, dkv_sem, uq_sem, uk_sem, cs_sem, cr_sem, ks_sem, kr_sem, qs_sem, qv_sem,
        c_sem, uv_sem, wo_sem, sa_sem, ra_sem, sb_sem, rb_sem, h_sem, p_sem, f_sem, g_sem):
    (n_req, heads, latent, nope, rope, v_dim, low, d_model, t_dev, t_chunk, n_dq, n_kv, n_uq, n_uk, grp, n_slots, n_split, scale) = dims
    f32, bf16 = jnp.float32, jnp.bfloat16
    nt = (((1,), (1,)), ((), ()))
    me = lax.axis_index('cp')
    core = lax.rem(me, 2)
    chip = me // 2
    partner = chip * 2 + (1 - core)
    hp = heads // 2
    hs = heads // 8
    my_head = core * hp + chip * hs
    n_lat = latent // 128
    lcols = low // 4
    kcols = latent // 4
    n_grp = hp // grp
    wide = grp * (nope + rope)
    drows = d_model // n_dq
    kdepth = d_model // n_kv
    krows = kcols + rope
    half_cols = d_model // 2
    qcols = d_model // 8
    n_wo = 8

    def peer_chip(d):
        return lax.rem(chip + d, 4)

    def from_chip(d):
        return lax.rem(chip + 4 - d, 4)

    def peer(d):
        return peer_chip(d) * 2 + core

    def dq_piece(i):
        return wo_buf.at[pl.ds(low, drows), pl.ds(i * lcols, lcols)]

    def dq_copy(i):
        return pltpu.make_async_copy(dq_hbm.at[pl.ds(i * drows, drows), pl.ds(pl.multiple_of(chip * lcols, lcols), lcols)], dq_piece(i), dq_sem.at[i])

    def kv_piece(i, row, rows):
        return wo_buf.at[pl.ds(i * krows + row, rows), pl.ds(n_uq * wide, kdepth)]

    def dkv_copies(i):
        cols = pl.ds(i * kdepth, kdepth)
        return [pltpu.make_async_copy(dkv_hbm.at[pl.ds(pl.multiple_of(chip * kcols, kcols), kcols), cols], kv_piece(i, 0, kcols), dkv_sem.at[0, i]),
                pltpu.make_async_copy(dkv_hbm.at[pl.ds(latent, rope), cols], kv_piece(i, kcols, rope), dkv_sem.at[1, i])]

    def uq_slot(g):
        return pl.ds(pl.multiple_of(lax.rem(g, n_uq) * wide, wide), wide)

    def grp_copies(g):
        head = core * hp + g * grp
        cols = pl.ds(pl.multiple_of(head * (nope + rope), wide), wide)
        half = low // 2
        slot = lax.rem(g, n_uq)
        return [pltpu.make_async_copy(uq_hbm.at[pl.ds(i * half, half), cols], wo_buf.at[pl.ds(i * half, half), uq_slot(g)], uq_sem.at[slot, i])
                for i in (0, 1)] + [
            pltpu.make_async_copy(uk_hbm.at[:, pl.ds(pl.multiple_of(head, grp), grp), :], uk_buf.at[lax.rem(g, n_uk)], uk_sem.at[lax.rem(g, n_uk)])]

    def c_copies(b):
        slot = lax.rem(b, n_slots)
        rows = t_dev // n_split
        out = []
        for i in range(n_split):
            sl = pl.ds(i * rows, rows)
            out.append(pltpu.make_async_copy(c_hbm.at[b, sl], c_buf.at[slot, sl], c_sem.at[slot, i]))
        out.append(pltpu.make_async_copy(kr_hbm.at[b], kr_buf.at[slot], c_sem.at[slot, n_split]))
        return out

    def uv_copy(i):
        return pltpu.make_async_copy(uv_hbm.at[:, pl.ds(pl.multiple_of(my_head + i * grp, grp), grp), :], uk_buf.at[i], uv_sem.at[i])

    def wo_block(i):
        half = jnp.where(i < 4, 1 - core, core)
        return half * half_cols + lax.rem(chip + 1 + i, 4) * qcols

    def wo_slot(i):
        return pl.ds(pl.multiple_of(i * qcols, qcols), qcols)

    def wo_copy(i):
        rows = pl.ds(pl.multiple_of(my_head * v_dim, hs * v_dim), hs * v_dim)
        return pltpu.make_async_copy(wo_hbm.at[rows, pl.ds(pl.multiple_of(wo_block(i), qcols), qcols)], wo_buf.at[:, wo_slot(i)], wo_sem.at[i])

    for i in range(n_dq):
        dq_copy(i).start()
    for i in range(n_kv):
        for cp in dkv_copies(i):
            cp.start()
    for g in range(n_uk - 1):
        for cp in grp_copies(g):
            cp.start()

    barrier = pltpu.get_barrier_semaphore()
    pl.semaphore_signal(barrier, inc=1, device_id={'cp': partner}, device_id_type=pl.DeviceIdType.MESH)
    for d in (1, 2, 3):
        pl.semaphore_signal(barrier, inc=1, device_id={'cp': peer(d)}, device_id_type=pl.DeviceIdType.MESH)

    cq = None
    for i in range(n_dq):
        dq_copy(i).wait()
        part = jnp.dot(x_ref[:, i * drows:(i + 1) * drows], wo_buf[low:low + drows, i * lcols:(i + 1) * lcols], preferred_element_type=f32)
        cq = part if cq is None else cq + part
    cq_ref[chip] = cq.astype(bf16).astype(f32)
    pl.semaphore_wait(barrier, 4)

    def send_cq(d):
        return exchange(cq_ref.at[chip], cq_ref.at[chip], cs_sem.at[d - 1], cr_sem.at[d - 1], peer(d))

    def recv_cq(d):
        return exchange(cq_ref.at[from_chip(d)], cq_ref.at[from_chip(d)], cs_sem.at[d - 1], cr_sem.at[d - 1], peer(d))

    def send_kv(d):
        return exchange(kv_ref.at[chip], kv_ref.at[chip], ks_sem.at[d - 1], kr_sem.at[d - 1], peer(d))

    def recv_kv(d):
        return exchange(kv_ref.at[from_chip(d)], kv_ref.at[from_chip(d)], ks_sem.at[d - 1], kr_sem.at[d - 1], peer(d))

    for d in (1, 2, 3):
        send_cq(d).start()

    kv = None
    for i in range(n_kv):
        for cp in dkv_copies(i):
            cp.wait()
        part = lax.dot_general(x_ref[:, i * kdepth:(i + 1) * kdepth], wo_buf[i * krows:(i + 1) * krows, n_uq * wide:n_uq * wide + kdepth],
                               nt, preferred_element_type=f32)
        kv = part if kv is None else kv + part
    kv_ref[chip] = kv[:, :kcols]
    cos, sin = tab_ref[:, :rope // 2], tab_ref[:, rope // 2:]

    def rotate(v):
        lo, hi = v[:, :rope // 2], v[:, rope // 2:]
        return jnp.concatenate([lo * cos - hi * sin, hi * cos + lo * sin], axis=1)

    kn_ref[...] = rotate(kv[:, kcols:kcols + rope]).astype(bf16).astype(f32)

    for d in (1, 2, 3):
        recv_cq(d).wait_recv()
    for d in (1, 2, 3):
        send_kv(d).start()

    def rms(parts):
        total = None
        for p in parts:
            sq = jnp.sum(p * p, axis=1, keepdims=True)
            total = sq if total is None else total + sq
        return lax.rsqrt(total * (1.0 / (len(parts) * parts[0].shape[1])) + NORM_EPS)

    inv = rms([cq_ref[i] for i in range(4)])
    for i in range(4):
        norm_ref[:, i * lcols:(i + 1) * lcols] = (cq_ref[i] * inv * gq_ref[:, i * lcols:(i + 1) * lcols]).astype(bf16)

    def q_rows(c, g):
        return pl.ds(pl.multiple_of((c * hp + g * grp) * n_req, grp * n_req), grp * n_req)

    def send_q(g):
        return exchange(q_ref.at[:, q_rows(core, g)], q_ref.at[:, q_rows(core, g)], qs_sem.at[g], qv_sem.at[g], partner)

    def recv_q(g):
        return exchange(q_ref.at[:, q_rows(1 - core, g)], q_ref.at[:, q_rows(1 - core, g)], qs_sem.at[g], qv_sem.at[g], partner)

    def group(g, carry):
        @pl.when(g + n_uk - 1 < n_grp)
        def _():
            for cp in grp_copies(g + n_uk - 1):
                cp.start()

        @pl.when(g >= n_grp - (n_slots - 1))
        def _():
            for cp in c_copies(g - (n_grp - (n_slots - 1))):
                cp.start()

        for cp in grp_copies(g):
            cp.wait()

        @pl.when(g >= 1)
        def _():
            send_q(g - 1).start()

        q = jnp.dot(norm_ref[...], wo_buf[:low, uq_slot(g)], preferred_element_type=f32).astype(bf16).astype(f32)
        s_ref[...] = uk_buf[lax.rem(g, n_uk)].astype(f32).reshape(latent * grp, nope)
        for h in range(grp):
            at = h * (nope + rope)
            turn_ref[h % 2, :nope, :] = s_ref[pl.ds(h, latent, stride=grp), :].astype(bf16).T
            lat = jnp.dot(q[:, at:at + nope].astype(bf16), turn_ref[h % 2, :nope, :], preferred_element_type=f32)
            rows = pl.ds(pl.multiple_of((core * hp + g * grp + h) * n_req, n_req), n_req)
            for j in range(n_lat):
                q_ref[j, rows, :] = lat[:, j * 128:(j + 1) * 128]
            rot = rotate(q[:, at + nope:at + nope + rope])
            q_ref[n_lat, rows, :] = jnp.concatenate([rot, jnp.zeros((n_req, 128 - rope), f32)], axis=1)
        return carry

    lax.fori_loop(0, n_grp, group, 0)
    send_q(n_grp - 1).start()

    for d in (1, 2, 3):
        recv_kv(d).wait_recv()
    inv = rms([kv_ref[i] for i in range(4)])
    for i in range(4):
        cn_ref[:, i * kcols:(i + 1) * kcols] = (kv_ref[i] * inv * gkv_ref[:, i * kcols:(i + 1) * kcols]).astype(bf16).astype(f32)
    for d in (1, 2, 3):
        send_cq(d).wait_send()
        send_kv(d).wait_send()

    def settle(g, carry):
        recv_q(g).wait_recv()
        return carry

    lax.fori_loop(0, n_grp, settle, 0)

    def send_a(b):
        slot = lax.rem(b, 2)
        return exchange(acc_buf.at[slot, pl.ds(pl.multiple_of((1 - core) * hp, hp), hp)], recv_a.at[slot], sa_sem.at[b], ra_sem.at[b], partner)

    def send_b(b, d):
        slot = lax.rem(b, 2)
        return exchange(comb.at[slot, pl.ds(pl.multiple_of(peer_chip(d) * hs, hs), hs)], recv_b.at[b, d - 1], sb_sem.at[b, d - 1],
                        rb_sem.at[b, d - 1], peer(d))

    def pair_merge(b):
        slot = lax.rem(b, 2)
        send_a(b).wait_recv()
        mine = acc_buf[slot, pl.ds(pl.multiple_of(core * hp, hp), hp), :]
        acc, top, mass = merge([mine, recv_a[slot]], latent)
        comb[slot, :, :latent] = acc
        comb[slot, :, latent:] = stats(top, mass)
        own_b[b] = comb[slot, pl.ds(pl.multiple_of(chip * hs, hs), hs), :]

    base = me * t_dev
    n_chunks = t_dev // t_chunk
    lanes = t_chunk // 128
    k2 = scale * LOG2E

    def step(b, carry):
        slot = lax.rem(b, n_slots)

        @pl.when(b + n_slots - 1 < n_req)
        def _():
            for cp in c_copies(b + n_slots - 1):
                cp.start()

        @pl.when(b < n_wo)
        def _():
            wo_copy(b).start()

        @pl.when(b == n_wo)
        def _():
            for i in range(hs // grp):
                uv_copy(i).start()

        for cp in c_copies(b):
            cp.wait()

        @pl.when(b >= 1)
        def _():
            send_a(b - 1).start()

        @pl.when(b >= 2)
        def _():
            for d in (1, 2, 3):
                send_b(b - 2, d).start()

        limit = ctx_ref[b] - base
        q = jnp.concatenate([q_ref[j, pl.ds(b, heads, stride=n_req), :].astype(bf16) for j in range(n_lat)], axis=1)
        qr = q_ref[n_lat, pl.ds(b, heads, stride=n_req), :][:, :rope].astype(bf16)
        top = None
        for i in range(n_chunks):
            sl = pl.ds(i * t_chunk, t_chunk)
            turn_ref[i % 2] = c_buf[slot, sl, :].T
            s = jnp.dot(q, turn_ref[i % 2], preferred_element_type=f32)
            s = s + jnp.dot(qr, kr_buf[slot, :, sl], preferred_element_type=f32)
            pos = lax.broadcasted_iota(jnp.int32, (1, t_chunk), 1) + i * t_chunk
            s = jnp.where(pos < limit, s, MASKED)
            for j in range(lanes):
                s_ref[pl.ds((i * lanes + j) * heads, heads), :] = s[:, j * 128:(j + 1) * 128]
            cm = jnp.max(s, axis=1, keepdims=True)
            top = cm if top is None else jnp.maximum(top, cm)
        top = jnp.maximum(top, FLOOR)
        acc, mass = None, None
        for i in range(n_chunks):
            sl = pl.ds(i * t_chunk, t_chunk)
            s = jnp.concatenate([s_ref[pl.ds((i * lanes + j) * heads, heads), :] for j in range(lanes)], axis=1)
            p = jnp.exp2((s - top) * k2)
            ls = jnp.sum(p, axis=1, keepdims=True)
            mass = ls if mass is None else mass + ls
            o = jnp.dot(p.astype(bf16), c_buf[slot, sl, :], preferred_element_type=f32)
            acc = o if acc is None else acc + o

        @pl.when(b >= 2)
        def _():
            send_a(b - 2).wait_send()

        @pl.when(b >= 3)
        def _():
            for d in (1, 2, 3):
                send_b(b - 3, d).wait_send()

        a_slot = lax.rem(b, 2)
        acc_buf[a_slot, :, :latent] = acc
        acc_buf[a_slot, :, latent:] = stats(top * scale, mass)

        @pl.when(b >= 1)
        def _():
            pair_merge(b - 1)

        return carry

    lax.fori_loop(0, n_req, step, 0)

    def final(b, carry):
        for d in (1, 2, 3):
            send_b(b, d).wait_recv()
        rows = pl.ds(my_head * n_req + b, hs, stride=n_req)
        cn = cn_ref[pl.ds(b, 1), :]
        s_new = jnp.sum(q_ref[n_lat, rows, :][:, :rope].astype(bf16).astype(f32) * kn_ref[pl.ds(b, 1), :], axis=1, keepdims=True)
        for j in range(n_lat):
            s_new = s_new + jnp.sum(q_ref[j, rows, :].astype(bf16).astype(f32) * cn[:, j * 128:(j + 1) * 128], axis=1, keepdims=True)
        s_new = s_new * scale
        parts = [own_b[b]] + [recv_b[b, d] for d in range(3)]
        tops = [p[:, latent:latent + 1] for p in parts] + [s_new]
        top = functools.reduce(jnp.maximum, tops)
        w_new = jnp.exp(s_new - top)
        mass = w_new
        acc = w_new.astype(bf16).astype(f32) * cn
        for p, t in zip(parts, tops):
            f = jnp.exp(t - top)
            acc = acc + p[:, :latent] * f
            mass = mass + p[:, latent + 64:latent + 65] * f
        o_lat = (acc / mass).astype(bf16).astype(f32)
        for j in range(n_lat):
            olat_ref[j, pl.ds(pl.multiple_of(b * hs, hs), hs), :] = o_lat[:, j * 128:(j + 1) * 128]
        return carry

    last = n_req - 1
    send_a(last).start()
    for d in (1, 2, 3):
        send_b(last - 1, d).start()
    lax.fori_loop(0, last - 1, final, 0)
    send_a(last - 1).wait_send()
    for d in (1, 2, 3):
        send_b(last - 2, d).wait_send()
    pair_merge(last)
    for i in range(hs // grp):
        uv_copy(i).wait()
        s_ref[...] = uk_buf[i].astype(f32).reshape(latent * grp, v_dim)
        if i == 0:
            for d in (1, 2, 3):
                send_b(last, d).start()
        for h in range(grp):
            c_buf[0, h * latent:(h + 1) * latent, i * v_dim:(i + 1) * v_dim] = s_ref[pl.ds(h, latent, stride=grp), :].astype(bf16)
    lax.fori_loop(last - 1, n_req, final, 0)
    send_a(last).wait_send()
    for b in (last - 1, last):
        for d in (1, 2, 3):
            send_b(b, d).wait_send()

    for h in range(hs):
        lhs = jnp.concatenate([olat_ref[j, pl.ds(h, n_req, stride=hs), :] for j in range(n_lat)], axis=1)
        uv = c_buf[0, (h % grp) * latent:(h % grp + 1) * latent, (h // grp) * v_dim:(h // grp + 1) * v_dim]
        o = jnp.dot(lhs.astype(bf16), uv, preferred_element_type=f32)
        o_ref[:, h * v_dim:(h + 1) * v_dim] = o.astype(bf16)

    def block(i):
        wo_copy(i).wait()
        return jnp.dot(o_ref[...], wo_buf[:, wo_slot(i)], preferred_element_type=f32)

    def to_pair(i):
        return exchange(po_ref.at[i], pair_ref.at[i], h_sem.at[0, i], h_sem.at[1, i], partner)

    def to_owner(i):
        return exchange(sum_ref.at[i], quart_ref.at[i], p_sem.at[0, i], p_sem.at[1, i], peer(i + 1))

    def first(i, carry):
        po_ref[i] = block(i)

        @pl.when(i >= 1)
        def _():
            to_pair(i - 1).start()

        return carry

    lax.fori_loop(0, 4, first, 0)
    to_pair(3).start()

    def second(i, carry):
        part = block(i + 4)
        to_pair(i).wait_recv()
        sum_ref[i] = part + pair_ref[i]

        @pl.when((i >= 1) & (i < 4))
        def _():
            to_owner(i - 1).start()

        return carry

    lax.fori_loop(0, 4, second, 0)
    for i in range(3):
        to_owner(i).wait_recv()
    my_cols = pl.ds(pl.multiple_of(core * half_cols + chip * qcols, qcols), qcols)
    total = sum_ref[3] + quart_ref[0] + quart_ref[1] + quart_ref[2]
    fin_ref[...] = (x_ref[:, my_cols].astype(f32) + total).astype(bf16).astype(f32)

    def to_all(d):
        return exchange(fin_ref, xo_ref.at[:, my_cols], f_sem.at[0, d - 1], f_sem.at[1, d - 1], peer(d))

    def from_all(d):
        cols = pl.ds(pl.multiple_of(core * half_cols + from_chip(d) * qcols, qcols), qcols)
        return exchange(fin_ref, xo_ref.at[:, cols], f_sem.at[0, d - 1], f_sem.at[1, d - 1], peer(d)), cols

    for d in (1, 2, 3):
        to_all(d).start()
    g0 = exchange(fin_ref, xo_ref.at[:, my_cols], g_sem.at[0, 0], g_sem.at[1, 0], partner)
    g0.start()
    out_ref[:, d_model:d_model + latent] = cn_ref[...]
    out_ref[:, d_model + latent:] = jnp.concatenate([kn_ref[...], jnp.zeros((n_req, 128 - rope), f32)], axis=1)
    fwd = [g0]
    for d in (1, 2, 3):
        got, cols = from_all(d)
        got.wait_recv()
        f = exchange(xo_ref.at[:, cols], xo_ref.at[:, cols], g_sem.at[0, d], g_sem.at[1, d], partner)
        f.start()
        fwd.append(f)
    for d in (1, 2, 3):
        to_all(d).wait_send()
    for i in range(3):
        to_owner(i).wait_send()
    for i in range(4):
        to_pair(i).wait_send()

    def settle_sent(g, carry):
        send_q(g).wait_send()
        return carry

    lax.fori_loop(0, n_grp, settle_sent, 0)
    for f in fwd:
        f.wait()
    xo_ref[:, my_cols] = fin_ref[...]
    out_ref[:, :d_model] = xo_ref[...]


def decode(x, w_dq, g_q, w_uq, w_dkv, g_kv, w_uk, w_uv, w_o, cache_c, cache_kr, ctx_len):
    n_req, d_model = x.shape
    latent, heads, nope = w_uk.shape
    rope = w_dkv.shape[1] - latent
    low = w_dq.shape[1]
    v_dim = w_uv.shape[2]
    t_dev = cache_c.shape[1]
    scale = (nope + rope) ** -0.5
    n_dq, n_kv, n_uq, n_uk, grp, n_slots, n_split, t_chunk = 14, 7, 4, 3, 8, 3, 4, 512
    f32, bf16 = jnp.float32, jnp.bfloat16
    dims = (n_req, heads, latent, nope, rope, v_dim, low, d_model, t_dev, t_chunk, n_dq, n_kv, n_uq, n_uk, grp, n_slots, n_split, scale)
    lane = jnp.arange(rope)
    inv_freq = ROPE_THETA ** (-2.0 * (lane % (rope // 2)).astype(f32) / rope)
    angles = ctx_len.astype(f32)[:, None] * inv_freq
    table = jnp.where(lane < rope // 2, jnp.cos(angles), jnp.sin(angles))
    hs = heads // 8
    hp = heads // 2
    tail = latent + 128
    qcols = d_model // 8
    n_grp = hp // grp
    vmem = pl.BlockSpec(memory_space=pltpu.VMEM)
    hbm = pl.BlockSpec(memory_space=pl.ANY)
    dma = pltpu.SemaphoreType.DMA
    out = pl.pallas_call(
        functools.partial(decode_body, dims),
        out_shape=jax.ShapeDtypeStruct((n_req, d_model + latent + 128), f32),
        in_specs=[pl.BlockSpec(memory_space=pltpu.SMEM)] + [vmem] * 4 + [hbm] * 8,
        out_specs=vmem,
        scratch_shapes=[
            pltpu.VMEM((hs * v_dim, d_model), bf16),
            pltpu.VMEM((n_uk, latent, grp, nope), bf16),
            pltpu.VMEM((t_dev * heads // 128, 128), f32),
            pltpu.VMEM((2, latent, t_chunk), bf16),
            pltpu.VMEM((4, n_req, low // 4), f32),
            pltpu.VMEM((4, n_req, latent // 4), f32),
            pltpu.VMEM((n_req, low), bf16),
            pltpu.VMEM((latent // 128 + 1, heads * n_req, 128), f32),
            pltpu.VMEM((n_req, latent), f32),
            pltpu.VMEM((n_req, rope), f32),
            pltpu.VMEM((n_slots, t_dev, latent), bf16),
            pltpu.VMEM((n_slots, rope, t_dev), bf16),
            pltpu.VMEM((2, heads, tail), f32),
            pltpu.VMEM((2, hp, tail), f32),
            pltpu.VMEM((2, hp, tail), f32),
            pltpu.VMEM((n_req, 3, hs, tail), f32),
            pltpu.VMEM((n_req, hs, tail), f32),
            pltpu.VMEM((latent // 128, n_req * hs, 128), f32),
            pltpu.VMEM((n_req, hs * v_dim), bf16),
            pltpu.VMEM((4, n_req, qcols), f32),
            pltpu.VMEM((4, n_req, qcols), f32),
            pltpu.VMEM((4, n_req, qcols), f32),
            pltpu.VMEM((3, n_req, qcols), f32),
            pltpu.VMEM((n_req, qcols), f32),
            pltpu.VMEM((n_req, d_model), f32),
            dma((n_dq,)), dma((2, n_kv)), dma((n_uq, 2)), dma((n_uk,)),
            dma((3,)), dma((3,)), dma((3,)), dma((3,)), dma((n_grp,)), dma((n_grp,)),
            dma((n_slots, n_split + 1)), dma((hs // grp,)), dma((8,)),
            dma((n_req,)), dma((n_req,)), dma((n_req, 3)), dma((n_req, 3)),
            dma((2, 4)), dma((2, 3)), dma((2, 3)), dma((2, 4)),
        ],
        compiler_params=pltpu.CompilerParams(
            vmem_limit_bytes=67043328, collective_id=0, has_side_effects=True),
        name='decode',
    )(ctx_len, x, g_q.reshape(1, low), g_kv.reshape(1, latent), table, w_dq, w_uq, jnp.swapaxes(w_dkv, 0, 1), w_uk,
      cache_c, jnp.swapaxes(cache_kr, 1, 2), w_uv, w_o)
    return out[:, :d_model].astype(bf16), out[:, d_model:d_model + latent].astype(bf16), out[:, d_model + latent:d_model + latent + rope].astype(bf16)


def solution(mesh):
    def decode_step(*args):
        return decode(*args)

    spec_rows = P('dp', None)
    spec_cache = P('dp', 'cp', None)
    in_specs = (spec_rows, P(), P(), P(), P(), P(), P(), P(), P(), spec_cache, spec_cache, P('dp'))
    out_specs = (spec_rows, spec_rows, spec_rows)
    return jax.shard_map(decode_step, mesh=mesh, in_specs=in_specs, out_specs=out_specs, check_vma=False)
```

profile of v0, /device:TPU:0, one launch (start us, length us, event | category | flops | bytes accessed | tf_op | source)
XLA Modules:
  0.0 99.2 jit_solution(1698496840938520550)
XLA Ops:
  0.6 0.7 convert_element_type.13
  1.3 1.3 %reshape.25.gq_ref = f32[1,1536]{1,0:T(1,128)} reshape(f32[1536]{0:T(1024)} %param.14) | data formatting | bytes 12288 | tf_op jit(solution)/shard_map/reshape | solution.py:548
  2.6 0.7 fusion.tab_ref
  3.3 92.9 %decode.1 = f32[16,7808]{1,0:T(8,128)} custom-call(s32[16]{0:T(128)} %ctx_ref.1, bf16[16,7168]{1,0:T(8,128)(2,1)} %x_ref.1, f32[1,1536]{1,0:T(1,128)} %reshape.25.gq_ref, f32[1,512]{1,0:T(1,128)} %bitcast.5, f32[16,64]{1,0:T(8,128)} %fusion.tab_ref, bf16[7168,1536]{1,0:T(8,128)(2,1)} %dq_hbm.1, bf16[1536,24576]{1,0:T(8,128)(2,1)} %uq_hbm.1, ...), custom_call_target="tpu_custom_call" | custom-call | tf_op jit(solution)/shard_map/decode/pallas_call | solution.py:508
  96.2 1.1 %convert.5 = bf16[16,7808]{1,0:T(8,128)(2,1)S(1)} convert(f32[16,7808]{1,0:T(8,128)} %decode.1) | non-fusion elementwise | flops 124928 | bytes 749568 | tf_op jit(solution)/shard_map/convert.2
  97.3 0.6 slice.17
  97.9 0.6 slice.16
  98.5 0.7 slice.15
  (2 shorter events, 0.0 us)
where the time goes:
time: 99.4 us; the launch traced here: 99.2 us
  Pallas kernels  92.9 us (93%)
  local copies, waits for them, and re-layouts  3.2 us (3%)
  other arithmetic  2.45 us (2%)
    pallas_call x1, Pallas kernels, decode(): pl.pallas_call(functools.partial(decode_body, dims), out_shape=jax.ShapeD...  92.9 us

commit v1 on v0

--- a/solution.py
+++ b/solution.py
@@ -38,9 +38,9 @@
 
 
 def decode_body(
-        dims, ctx_ref, x_ref, gq_ref, gkv_ref, tab_ref, dq_hbm, uq_hbm, dkv_hbm, uk_hbm, c_hbm, kr_hbm, uv_hbm, wo_hbm, out_ref,
+        dims, c_buf, kr_buf, ctx_ref, x_ref, gq_ref, gkv_ref, tab_ref, dq_hbm, uq_hbm, dkv_hbm, uk_hbm, c_hbm, kr_hbm, uv_hbm, wo_hbm, out_ref, cno_ref, kno_ref,
         wo_buf, uk_buf, s_ref, turn_ref, cq_ref, kv_ref, norm_ref, q_ref, cn_ref, kn_ref,
-        c_buf, kr_buf, acc_buf, recv_a, comb, recv_b, own_b, olat_ref, o_ref,
+        acc_buf, recv_a, comb, recv_b, own_b, olat_ref, o_ref,
         po_ref, pair_ref, sum_ref, quart_ref, fin_ref, xo_ref,
         dq_sem, dkv_sem, uq_sem, uk_sem, cs_sem, cr_sem, ks_sem, kr_sem, qs_sem, qv_sem,
         c_sem, uv_sem, wo_sem, sa_sem, ra_sem, sb_sem, rb_sem, h_sem, p_sem, f_sem, g_sem):
@@ -192,7 +192,7 @@
 
     inv = rms([cq_ref[i] for i in range(4)])
     for i in range(4):
-        norm_ref[:, i * lcols:(i + 1) * lcols] = (cq_ref[i] * inv * gq_ref[:, i * lcols:(i + 1) * lcols]).astype(bf16)
+        norm_ref[:, i * lcols:(i + 1) * lcols] = (cq_ref[i] * inv * gq_ref[i * lcols:(i + 1) * lcols].reshape(1, lcols)).astype(bf16)
 
     def q_rows(c, g):
         return pl.ds(pl.multiple_of((c * hp + g * grp) * n_req, grp * n_req), grp * n_req)
@@ -241,7 +241,7 @@
         recv_kv(d).wait_recv()
     inv = rms([kv_ref[i] for i in range(4)])
     for i in range(4):
-        cn_ref[:, i * kcols:(i + 1) * kcols] = (kv_ref[i] * inv * gkv_ref[:, i * kcols:(i + 1) * kcols]).astype(bf16).astype(f32)
+        cn_ref[:, i * kcols:(i + 1) * kcols] = (kv_ref[i] * inv * gkv_ref[i * kcols:(i + 1) * kcols].reshape(1, kcols)).astype(bf16).astype(f32)
     for d in (1, 2, 3):
         send_cq(d).wait_send()
         send_kv(d).wait_send()
@@ -283,11 +283,13 @@
             for cp in c_copies(b + n_slots - 1):
                 cp.start()
 
-        @pl.when(b < n_wo)
-        def _():
-            wo_copy(b).start()
-
-        @pl.when(b == n_wo)
+        for first_wo, at in ((0, 3), (3, 2), (6, 1)):
+            @pl.when(b == n_req - at)
+            def _():
+                for i in range(first_wo, min(first_wo + 3, n_wo)):
+                    wo_copy(i).start()
+
+        @pl.when(b == n_req - 4)
         def _():
             for i in range(hs // grp):
                 uv_copy(i).start()
@@ -455,8 +457,8 @@
         to_all(d).start()
     g0 = exchange(fin_ref, xo_ref.at[:, my_cols], g_sem.at[0, 0], g_sem.at[1, 0], partner)
     g0.start()
-    out_ref[:, d_model:d_model + latent] = cn_ref[...]
-    out_ref[:, d_model + latent:] = jnp.concatenate([kn_ref[...], jnp.zeros((n_req, 128 - rope), f32)], axis=1)
+    cno_ref[...] = cn_ref[...]
+    kno_ref[...] = kn_ref[...]
     fwd = [g0]
     for d in (1, 2, 3):
         got, cols = from_all(d)
@@ -479,7 +481,14 @@
     for f in fwd:
         f.wait()
     xo_ref[:, my_cols] = fin_ref[...]
-    out_ref[:, :d_model] = xo_ref[...]
+    out_ref[...] = xo_ref[...]
+
+
+def scoped_body(dims, *refs):
+    latent, rope, t_dev, n_slots = dims[2], dims[4], dims[8], dims[15]
+    pl.run_scoped(
+        lambda c_buf, kr_buf: decode_body(dims, c_buf, kr_buf, *refs),
+        pltpu.VMEM((n_slots, t_dev, latent), jnp.bfloat16), pltpu.VMEM((n_slots, rope, t_dev), jnp.bfloat16))
 
 
 def decode(x, w_dq, g_q, w_uq, w_dkv, g_kv, w_uk, w_uv, w_o, cache_c, cache_kr, ctx_len):
@@ -506,10 +515,10 @@
     hbm = pl.BlockSpec(memory_space=pl.ANY)
     dma = pltpu.SemaphoreType.DMA
     out = pl.pallas_call(
-        functools.partial(decode_body, dims),
-        out_shape=jax.ShapeDtypeStruct((n_req, d_model + latent + 128), f32),
+        functools.partial(scoped_body, dims),
+        out_shape=[jax.ShapeDtypeStruct((n_req, n), f32) for n in (d_model, latent, rope)],
         in_specs=[pl.BlockSpec(memory_space=pltpu.SMEM)] + [vmem] * 4 + [hbm] * 8,
-        out_specs=vmem,
+        out_specs=[vmem] * 3,
         scratch_shapes=[
             pltpu.VMEM((hs * v_dim, d_model), bf16),
             pltpu.VMEM((n_uk, latent, grp, nope), bf16),
@@ -521,8 +530,6 @@
             pltpu.VMEM((latent // 128 + 1, heads * n_req, 128), f32),
             pltpu.VMEM((n_req, latent), f32),
             pltpu.VMEM((n_req, rope), f32),
-            pltpu.VMEM((n_slots, t_dev, latent), bf16),
-            pltpu.VMEM((n_slots, rope, t_dev), bf16),
             pltpu.VMEM((2, heads, tail), f32),
             pltpu.VMEM((2, hp, tail), f32),
             pltpu.VMEM((2, hp, tail), f32),
@@ -545,9 +552,9 @@
         compiler_params=pltpu.CompilerParams(
             vmem_limit_bytes=67043328, collective_id=0, has_side_effects=True),
         name='decode',
-    )(ctx_len, x, g_q.reshape(1, low), g_kv.reshape(1, latent), table, w_dq, w_uq, jnp.swapaxes(w_dkv, 0, 1), w_uk,
+    )(ctx_len, x, g_q, g_kv, table, w_dq, w_uq, jnp.swapaxes(w_dkv, 0, 1), w_uk,
       cache_c, jnp.swapaxes(cache_kr, 1, 2), w_uv, w_o)
-    return out[:, :d_model].astype(bf16), out[:, d_model:d_model + latent].astype(bf16), out[:, d_model + latent:d_model + latent + rope].astype(bf16)
+    return tuple(o.astype(bf16) for o in out)
 
 
 def solution(mesh):

time: 99.4 us -> 99.8 us (level)
  other arithmetic: 2.45 us -> 5.78 us
  local copies, waits for them, and re-layouts: 3.2 us -> 0 us
    convert_element_type x0 -> x3, other arithmetic: none -> 4.39 us  [decode(): return tuple((o.astype(bf16) for o in out))]
    slice x3 -> x0, local copies, waits for them, and re-layouts: 1.9 us -> none  [the longest x1 0.7 us: decode(): out[:, :d_model].astype(bf16)]
    reshape x1 -> x0, local copies, waits for them, and re-layouts: 1.3 us -> none  [decode(): g_q.reshape(1, low)]
    another operation x1 -> x0, other arithmetic: 1.06 us -> none
where the time goes in v1:
time: 99.8 us; the launch traced here: 99.5 us
  Pallas kernels  93.1 us (93%)
  other arithmetic  5.78 us (6%)
    pallas_call x1, Pallas kernels, decode(): pl.pallas_call(functools.partial(scoped_body, dims), out_shape=[jax.Shape...  93.1 us
    convert_element_type x3, other arithmetic, decode(): return tuple((o.astype(bf16) for o in out))  4.39 us

profile of v1, /device:TPU:0, one launch (start us, length us, event | category | flops | bytes accessed | tf_op | source)
XLA Modules:
  0.0 99.5 jit_solution(18423560440833097413)
XLA Ops:
  0.6 0.7 convert_element_type.19
  1.3 0.7 fusion.refs_4_
  2.0 93.1 %decode.1 = (f32[16,7168]{1,0:T(8,128)}, f32[16,512]{1,0:T(8,128)}, f32[16,64]{1,0:T(8,128)}) custom-call(s32[16]{0:T(128)} %refs_0_.1, bf16[16,7168]{1,0:T(8,128)(2,1)} %refs_1_.1, f32[1536]{0:T(1024)} %refs_2_.1, f32[512]{0:T(512)} %refs_3_.1, f32[16,64]{1,0:T(8,128)} %fusion.refs_4_, bf16[7168,1536]{1,0:T(8,128)(2,1)} %refs_5_.1, ...), custom_call_target="tpu_custom_call" | custom-call | tf_op jit(solution)/shard_map/decode/pallas_call | solution.py:517
  95.1 1.7 %convert_element_type.21 = bf16[16,7168]{1,0:T(8,128)(2,1)} convert(f32[16,7168]{1,0:T(8,128)} %get-tuple-element.6) | non-fusion elementwise | flops 114688 | bytes 688128 | tf_op jit(solution)/shard_map/convert_element_type | solution.py:557
  96.8 1.3 %convert_element_type.23 = bf16[16,64]{1,0:T(8,128)(2,1)} convert(f32[16,64]{1,0:T(8,128)} %get-tuple-element.8) | non-fusion elementwise | flops 1024 | bytes 6144 | tf_op jit(solution)/shard_map/convert_element_type | solution.py:557
  98.1 1.4 %convert_element_type.22 = bf16[16,512]{1,0:T(8,128)(2,1)} convert(f32[16,512]{1,0:T(8,128)} %get-tuple-element.7) | non-fusion elementwise | flops 8192 | bytes 49152 | tf_op jit(solution)/shard_map/convert_element_type | solution.py:557
  (2 shorter events, 0.0 us)

commit v2 on v1

--- a/solution.py
+++ b/solution.py
@@ -38,8 +38,8 @@
 
 
 def decode_body(
-        dims, c_buf, kr_buf, ctx_ref, x_ref, gq_ref, gkv_ref, tab_ref, dq_hbm, uq_hbm, dkv_hbm, uk_hbm, c_hbm, kr_hbm, uv_hbm, wo_hbm, out_ref, cno_ref, kno_ref,
-        wo_buf, uk_buf, s_ref, turn_ref, cq_ref, kv_ref, norm_ref, q_ref, cn_ref, kn_ref,
+        dims, c_buf, kr_buf, p_ref, turn_ref, ctx_ref, x_ref, gq_ref, gkv_ref, tab_ref, dq_hbm, uq_hbm, dkv_hbm, uk_hbm, c_hbm, kr_hbm, uv_hbm, wo_hbm, out_ref,
+        wo_buf, uk_buf, s_ref, top_ref, cq_ref, kv_ref, norm_ref, q_ref, cn_ref, kn_ref,
         acc_buf, recv_a, comb, recv_b, own_b, olat_ref, o_ref,
         po_ref, pair_ref, sum_ref, quart_ref, fin_ref, xo_ref,
         dq_sem, dkv_sem, uq_sem, uk_sem, cs_sem, cr_sem, ks_sem, kr_sem, qs_sem, qv_sem,
@@ -92,23 +92,26 @@
     def uq_slot(g):
         return pl.ds(pl.multiple_of(lax.rem(g, n_uq) * wide, wide), wide)
 
-    def grp_copies(g):
-        head = core * hp + g * grp
-        cols = pl.ds(pl.multiple_of(head * (nope + rope), wide), wide)
+    def uq_copies(g):
+        cols = pl.ds(pl.multiple_of((core * hp + g * grp) * (nope + rope), wide), wide)
         half = low // 2
         slot = lax.rem(g, n_uq)
         return [pltpu.make_async_copy(uq_hbm.at[pl.ds(i * half, half), cols], wo_buf.at[pl.ds(i * half, half), uq_slot(g)], uq_sem.at[slot, i])
-                for i in (0, 1)] + [
-            pltpu.make_async_copy(uk_hbm.at[:, pl.ds(pl.multiple_of(head, grp), grp), :], uk_buf.at[lax.rem(g, n_uk)], uk_sem.at[lax.rem(g, n_uk)])]
-
-    def c_copies(b):
+                for i in (0, 1)]
+
+    def uk_copy(g):
+        slot = lax.rem(g, n_uk)
+        return pltpu.make_async_copy(uk_hbm.at[:, pl.ds(pl.multiple_of(core * hp + g * grp, grp), grp), :], uk_buf.at[slot], uk_sem.at[slot])
+
+    def c_copies(b, half):
         slot = lax.rem(b, n_slots)
         rows = t_dev // n_split
         out = []
-        for i in range(n_split):
+        for i in range(half * n_split // 2, (half + 1) * n_split // 2):
             sl = pl.ds(i * rows, rows)
             out.append(pltpu.make_async_copy(c_hbm.at[b, sl], c_buf.at[slot, sl], c_sem.at[slot, i]))
-        out.append(pltpu.make_async_copy(kr_hbm.at[b], kr_buf.at[slot], c_sem.at[slot, n_split]))
+        if half == 0:
+            out.append(pltpu.make_async_copy(kr_hbm.at[b], kr_buf.at[slot], c_sem.at[slot, n_split]))
         return out
 
     def uv_copy(i):
@@ -130,8 +133,9 @@
     for i in range(n_kv):
         for cp in dkv_copies(i):
             cp.start()
-    for g in range(n_uk - 1):
-        for cp in grp_copies(g):
+    uk_copy(0).start()
+    for g in range(n_uq - 1):
+        for cp in uq_copies(g):
             cp.start()
 
     barrier = pltpu.get_barrier_semaphore()
@@ -204,18 +208,23 @@
         return exchange(q_ref.at[:, q_rows(1 - core, g)], q_ref.at[:, q_rows(1 - core, g)], qs_sem.at[g], qv_sem.at[g], partner)
 
     def group(g, carry):
-        @pl.when(g + n_uk - 1 < n_grp)
-        def _():
-            for cp in grp_copies(g + n_uk - 1):
+        @pl.when(g + 1 < n_grp)
+        def _():
+            uk_copy(g + 1).start()
+
+        @pl.when(g + n_uq - 1 < n_grp)
+        def _():
+            for cp in uq_copies(g + n_uq - 1):
                 cp.start()
 
-        @pl.when(g >= n_grp - (n_slots - 1))
-        def _():
-            for cp in c_copies(g - (n_grp - (n_slots - 1))):
+        @pl.when(g >= n_grp - n_slots)
+        def _():
+            for cp in c_copies(g - (n_grp - n_slots), 0) + c_copies(g - (n_grp - n_slots), 1):
                 cp.start()
 
-        for cp in grp_copies(g):
+        for cp in uq_copies(g):
             cp.wait()
+        uk_copy(g).wait()
 
         @pl.when(g >= 1)
         def _():
@@ -225,8 +234,8 @@
         s_ref[...] = uk_buf[lax.rem(g, n_uk)].astype(f32).reshape(latent * grp, nope)
         for h in range(grp):
             at = h * (nope + rope)
-            turn_ref[h % 2, :nope, :] = s_ref[pl.ds(h, latent, stride=grp), :].astype(bf16).T
-            lat = jnp.dot(q[:, at:at + nope].astype(bf16), turn_ref[h % 2, :nope, :], preferred_element_type=f32)
+            turn_ref[h % 2, :nope, :latent] = s_ref[pl.ds(h, latent, stride=grp), :].astype(bf16).T
+            lat = jnp.dot(q[:, at:at + nope].astype(bf16), turn_ref[h % 2, :nope, :latent], preferred_element_type=f32)
             rows = pl.ds(pl.multiple_of((core * hp + g * grp + h) * n_req, n_req), n_req)
             for j in range(n_lat):
                 q_ref[j, rows, :] = lat[:, j * 128:(j + 1) * 128]
@@ -275,14 +284,85 @@
     lanes = t_chunk // 128
     k2 = scale * LOG2E
 
+    def query(b):
+        q = jnp.concatenate([q_ref[j, pl.ds(b, heads, stride=n_req), :].astype(bf16) for j in range(n_lat)], axis=1)
+        return q, q_ref[n_lat, pl.ds(b, heads, stride=n_req), :][:, :rope].astype(bf16), ctx_ref[b] - base
+
+    def scores(b, query_b, i):
+        q, qr, limit = query_b
+        slot = lax.rem(b, n_slots)
+        sl = pl.ds(i * t_chunk, t_chunk)
+        turn_ref[i % 2, :, :t_chunk] = c_buf[slot, sl, :].T
+        s = jnp.dot(q, turn_ref[i % 2, :, :t_chunk], preferred_element_type=f32)
+        s = s + jnp.dot(qr, kr_buf[slot, :, sl], preferred_element_type=f32)
+        pos = lax.broadcasted_iota(jnp.int32, (1, t_chunk), 1) + i * t_chunk
+        s = jnp.where(pos < limit, s, MASKED)
+        top = None
+        for j in range(lanes):
+            part = s[:, j * 128:(j + 1) * 128]
+            s_ref[pl.ds((i * lanes + j) * heads, heads), :] = part
+            top = part if top is None else jnp.maximum(top, part)
+        return top
+
+    def weigh(top, i):
+        mass = None
+        for j in range(lanes):
+            p = jnp.exp2((s_ref[pl.ds((i * lanes + j) * heads, heads), :] - top) * k2)
+            mass = p if mass is None else mass + p
+            p_ref[:, (i * lanes + j) * 128:(i * lanes + j + 1) * 128] = p.astype(bf16)
+        return mass
+
+    def values(b, i):
+        sl = pl.ds(i * t_chunk, t_chunk)
+        return jnp.dot(p_ref[:, sl], c_buf[lax.rem(b, n_slots), sl, :], preferred_element_type=f32)
+
+    def add(a, v):
+        return v if a is None else a + v
+
+    def top_of(a):
+        return jnp.maximum(jnp.max(a, axis=1, keepdims=True), FLOOR)
+
+    def release(r):
+        @pl.when(r >= 1)
+        def _():
+            send_a(r - 1).start()
+
+        @pl.when(r >= 2)
+        def _():
+            for d in (1, 2, 3):
+                send_b(r - 2, d).start()
+
+    def settle_partial(r, acc, top, mass):
+        @pl.when(r >= 2)
+        def _():
+            send_a(r - 2).wait_send()
+
+        @pl.when(r >= 3)
+        def _():
+            for d in (1, 2, 3):
+                send_b(r - 3, d).wait_send()
+
+        a_slot = lax.rem(r, 2)
+        acc_buf[a_slot, :, :latent] = acc
+        acc_buf[a_slot, :, latent:] = stats(top * scale, jnp.sum(mass, axis=1, keepdims=True))
+
+        @pl.when(r >= 1)
+        def _():
+            pair_merge(r - 1)
+
+    for half in (0, 1):
+        for cp in c_copies(0, half):
+            cp.wait()
+    top = None
+    query_0 = query(0)
+    for i in range(n_chunks):
+        t = scores(0, query_0, i)
+        top = t if top is None else jnp.maximum(top, t)
+    top_ref[...] = top_of(top) + jnp.zeros((heads, 128), f32)
+
     def step(b, carry):
-        slot = lax.rem(b, n_slots)
-
-        @pl.when(b + n_slots - 1 < n_req)
-        def _():
-            for cp in c_copies(b + n_slots - 1):
-                cp.start()
-
+        r = b - 1
+        release(r)
         for first_wo, at in ((0, 3), (3, 2), (6, 1)):
             @pl.when(b == n_req - at)
             def _():
@@ -294,64 +374,35 @@
             for i in range(hs // grp):
                 uv_copy(i).start()
 
-        for cp in c_copies(b):
-            cp.wait()
-
-        @pl.when(b >= 1)
-        def _():
-            send_a(b - 1).start()
-
-        @pl.when(b >= 2)
-        def _():
-            for d in (1, 2, 3):
-                send_b(b - 2, d).start()
-
-        limit = ctx_ref[b] - base
-        q = jnp.concatenate([q_ref[j, pl.ds(b, heads, stride=n_req), :].astype(bf16) for j in range(n_lat)], axis=1)
-        qr = q_ref[n_lat, pl.ds(b, heads, stride=n_req), :][:, :rope].astype(bf16)
-        top = None
-        for i in range(n_chunks):
-            sl = pl.ds(i * t_chunk, t_chunk)
-            turn_ref[i % 2] = c_buf[slot, sl, :].T
-            s = jnp.dot(q, turn_ref[i % 2], preferred_element_type=f32)
-            s = s + jnp.dot(qr, kr_buf[slot, :, sl], preferred_element_type=f32)
-            pos = lax.broadcasted_iota(jnp.int32, (1, t_chunk), 1) + i * t_chunk
-            s = jnp.where(pos < limit, s, MASKED)
-            for j in range(lanes):
-                s_ref[pl.ds((i * lanes + j) * heads, heads), :] = s[:, j * 128:(j + 1) * 128]
-            cm = jnp.max(s, axis=1, keepdims=True)
-            top = cm if top is None else jnp.maximum(top, cm)
-        top = jnp.maximum(top, FLOOR)
-        acc, mass = None, None
-        for i in range(n_chunks):
-            sl = pl.ds(i * t_chunk, t_chunk)
-            s = jnp.concatenate([s_ref[pl.ds((i * lanes + j) * heads, heads), :] for j in range(lanes)], axis=1)
-            p = jnp.exp2((s - top) * k2)
-            ls = jnp.sum(p, axis=1, keepdims=True)
-            mass = ls if mass is None else mass + ls
-            o = jnp.dot(p.astype(bf16), c_buf[slot, sl, :], preferred_element_type=f32)
-            acc = o if acc is None else acc + o
-
-        @pl.when(b >= 2)
-        def _():
-            send_a(b - 2).wait_send()
-
-        @pl.when(b >= 3)
-        def _():
-            for d in (1, 2, 3):
-                send_b(b - 3, d).wait_send()
-
-        a_slot = lax.rem(b, 2)
-        acc_buf[a_slot, :, :latent] = acc
-        acc_buf[a_slot, :, latent:] = stats(top * scale, mass)
-
-        @pl.when(b >= 1)
-        def _():
-            pair_merge(b - 1)
-
+        old = top_ref[...]
+        query_b = query(b)
+        top, mass, acc = None, None, None
+        for half in (0, 1):
+            for cp in c_copies(b, half):
+                cp.wait()
+            for i in range(half * n_chunks // 2, (half + 1) * n_chunks // 2):
+                mass = add(mass, weigh(old, i))
+                t = scores(b, query_b, i)
+                top = t if top is None else jnp.maximum(top, t)
+                acc = add(acc, values(r, i))
+
+            @pl.when(b + 2 < n_req)
+            def _():
+                for cp in c_copies(b + 2, half):
+                    cp.start()
+
+        top_ref[...] = top_of(top) + jnp.zeros((heads, 128), f32)
+        settle_partial(r, acc, old[:, :1], mass)
         return carry
 
-    lax.fori_loop(0, n_req, step, 0)
+    lax.fori_loop(1, n_req, step, 0)
+    release(n_req - 1)
+    old = top_ref[...]
+    mass, acc = None, None
+    for i in range(n_chunks):
+        mass = add(mass, weigh(old, i))
+        acc = add(acc, values(n_req - 1, i))
+    settle_partial(n_req - 1, acc, old[:, :1], mass)
 
     def final(b, carry):
         for d in (1, 2, 3):
@@ -457,8 +508,8 @@
         to_all(d).start()
     g0 = exchange(fin_ref, xo_ref.at[:, my_cols], g_sem.at[0, 0], g_sem.at[1, 0], partner)
     g0.start()
-    cno_ref[...] = cn_ref[...]
-    kno_ref[...] = kn_ref[...]
+    out_ref[:, d_model:d_model + latent] = cn_ref[...]
+    out_ref[:, d_model + latent:] = jnp.concatenate([kn_ref[...], jnp.zeros((n_req, 128 - rope), f32)], axis=1)
     fwd = [g0]
     for d in (1, 2, 3):
         got, cols = from_all(d)
@@ -481,14 +532,15 @@
     for f in fwd:
         f.wait()
     xo_ref[:, my_cols] = fin_ref[...]
-    out_ref[...] = xo_ref[...]
+    out_ref[:, :d_model] = xo_ref[...]
 
 
 def scoped_body(dims, *refs):
-    latent, rope, t_dev, n_slots = dims[2], dims[4], dims[8], dims[15]
+    heads, latent, rope, t_dev, t_chunk, n_slots = dims[1], dims[2], dims[4], dims[8], dims[9], dims[15]
     pl.run_scoped(
-        lambda c_buf, kr_buf: decode_body(dims, c_buf, kr_buf, *refs),
-        pltpu.VMEM((n_slots, t_dev, latent), jnp.bfloat16), pltpu.VMEM((n_slots, rope, t_dev), jnp.bfloat16))
+        lambda *scoped: decode_body(dims, *scoped, *refs),
+        pltpu.VMEM((n_slots, t_dev, latent), jnp.bfloat16), pltpu.VMEM((n_slots, rope, t_dev), jnp.bfloat16),
+        pltpu.VMEM((heads, t_dev), jnp.bfloat16), pltpu.VMEM((2, latent, max(t_chunk, latent)), jnp.bfloat16))
 
 
 def decode(x, w_dq, g_q, w_uq, w_dkv, g_kv, w_uk, w_uv, w_o, cache_c, cache_kr, ctx_len):
@@ -499,13 +551,14 @@
     v_dim = w_uv.shape[2]
     t_dev = cache_c.shape[1]
     scale = (nope + rope) ** -0.5
-    n_dq, n_kv, n_uq, n_uk, grp, n_slots, n_split, t_chunk = 14, 7, 4, 3, 8, 3, 4, 512
+    n_dq, n_kv, n_uq, n_uk, grp, n_slots, n_split, t_chunk = 14, 7, 4, 2, 8, 3, 4, 512
     f32, bf16 = jnp.float32, jnp.bfloat16
     dims = (n_req, heads, latent, nope, rope, v_dim, low, d_model, t_dev, t_chunk, n_dq, n_kv, n_uq, n_uk, grp, n_slots, n_split, scale)
     lane = jnp.arange(rope)
     inv_freq = ROPE_THETA ** (-2.0 * (lane % (rope // 2)).astype(f32) / rope)
     angles = ctx_len.astype(f32)[:, None] * inv_freq
     table = jnp.where(lane < rope // 2, jnp.cos(angles), jnp.sin(angles))
+    turn = max(t_chunk, latent)
     hs = heads // 8
     hp = heads // 2
     tail = latent + 128
@@ -516,14 +569,14 @@
     dma = pltpu.SemaphoreType.DMA
     out = pl.pallas_call(
         functools.partial(scoped_body, dims),
-        out_shape=[jax.ShapeDtypeStruct((n_req, n), f32) for n in (d_model, latent, rope)],
+        out_shape=jax.ShapeDtypeStruct((n_req, d_model + latent + 128), f32),
         in_specs=[pl.BlockSpec(memory_space=pltpu.SMEM)] + [vmem] * 4 + [hbm] * 8,
-        out_specs=[vmem] * 3,
+        out_specs=vmem,
         scratch_shapes=[
             pltpu.VMEM((hs * v_dim, d_model), bf16),
             pltpu.VMEM((n_uk, latent, grp, nope), bf16),
             pltpu.VMEM((t_dev * heads // 128, 128), f32),
-            pltpu.VMEM((2, latent, t_chunk), bf16),
+            pltpu.VMEM((heads, 128), f32),
             pltpu.VMEM((4, n_req, low // 4), f32),
             pltpu.VMEM((4, n_req, latent // 4), f32),
             pltpu.VMEM((n_req, low), bf16),
@@ -554,7 +607,7 @@
         name='decode',
     )(ctx_len, x, g_q, g_kv, table, w_dq, w_uq, jnp.swapaxes(w_dkv, 0, 1), w_uk,
       cache_c, jnp.swapaxes(cache_kr, 1, 2), w_uv, w_o)
-    return tuple(o.astype(bf16) for o in out)
+    return out[:, :d_model].astype(bf16), out[:, d_model:d_model + latent].astype(bf16), out[:, d_model + latent:d_model + latent + rope].astype(bf16)
 
 
 def solution(mesh):

time: 99.8 us -> 99.2 us (level)
  other arithmetic: 5.78 us -> 2.46 us
  local copies, waits for them, and re-layouts: 0 us -> 1.9 us
    convert_element_type x3 -> x0, other arithmetic: 4.39 us -> none  [decode(): return tuple((o.astype(bf16) for o in out))]
    slice x0 -> x3, local copies, waits for them, and re-layouts: none -> 1.9 us  [the longest x1 0.7 us: decode(): out[:, :d_model].astype(bf16)]
    another operation x0 -> x1, other arithmetic: none -> 1.06 us
where the time goes in v2:
time: 99.2 us; the launch traced here: 99 us
  Pallas kernels  94 us (95%)
  other arithmetic  2.46 us (2%)
  local copies, waits for them, and re-layouts  1.9 us (2%)
    pallas_call x1, Pallas kernels, decode(): pl.pallas_call(functools.partial(scoped_body, dims), out_shape=jax.ShapeD...  94 us

profile of v2, /device:TPU:0, one launch (start us, length us, event | category | flops | bytes accessed | tf_op | source)
XLA Modules:
  0.0 99.0 jit_solution(6435453999654483549)
XLA Ops:
  0.6 0.7 convert_element_type.13
  1.3 0.7 fusion.refs_4_
  2.0 94.0 %decode.1 = f32[16,7808]{1,0:T(8,128)} custom-call(s32[16]{0:T(128)} %refs_0_.1, bf16[16,7168]{1,0:T(8,128)(2,1)} %refs_1_.1, f32[1536]{0:T(1024)} %refs_2_.1, f32[512]{0:T(512)} %refs_3_.1, f32[16,64]{1,0:T(8,128)} %fusion.refs_4_, bf16[7168,1536]{1,0:T(8,128)(2,1)} %refs_5_.1, bf16[1536,24576]{1,0:T(8,128)(2,1)} %refs_6_.1, bf16[576,7168]{1,0:T(8,128)(2,1)} %bitcast.3, ...), custom_call_target="tpu_custom_call" | custom-call | tf_op jit(solution)/shard_map/decode/pallas_call | solution.py:570
  96.0 1.1 %convert.5 = bf16[16,7808]{1,0:T(8,128)(2,1)S(1)} convert(f32[16,7808]{1,0:T(8,128)} %decode.1) | non-fusion elementwise | flops 124928 | bytes 749568 | tf_op jit(solution)/shard_map/convert.2
  97.1 0.6 slice.17
  97.7 0.6 slice.16
  98.3 0.7 slice.15
  (2 shorter events, 0.0 us)

commit v3 on v2

--- a/solution.py
+++ b/solution.py
@@ -38,7 +38,7 @@
 
 
 def decode_body(
-        dims, c_buf, kr_buf, p_ref, turn_ref, ctx_ref, x_ref, gq_ref, gkv_ref, tab_ref, dq_hbm, uq_hbm, dkv_hbm, uk_hbm, c_hbm, kr_hbm, uv_hbm, wo_hbm, out_ref,
+        dims, c_buf, kr_buf, p_ref, turn_ref, qs_ref, ctx_ref, x_ref, gq_ref, gkv_ref, tab_ref, dq_hbm, uq_hbm, dkv_hbm, uk_hbm, c_hbm, kr_hbm, uv_hbm, wo_hbm, out_ref,
         wo_buf, uk_buf, s_ref, top_ref, cq_ref, kv_ref, norm_ref, q_ref, cn_ref, kn_ref,
         acc_buf, recv_a, comb, recv_b, own_b, olat_ref, o_ref,
         po_ref, pair_ref, sum_ref, quart_ref, fin_ref, xo_ref,
@@ -118,8 +118,9 @@
         return pltpu.make_async_copy(uv_hbm.at[:, pl.ds(pl.multiple_of(my_head + i * grp, grp), grp), :], uk_buf.at[i], uv_sem.at[i])
 
     def wo_block(i):
-        half = jnp.where(i < 4, 1 - core, core)
-        return half * half_cols + lax.rem(chip + 1 + i, 4) * qcols
+        half = jnp.where((i < 3) | (i == 6), 1 - core, core)
+        d = jnp.where(i < 3, i + 1, jnp.where(i < 6, i - 2, 0))
+        return half * half_cols + lax.rem(chip + d, 4) * qcols
 
     def wo_slot(i):
         return pl.ds(pl.multiple_of(i * qcols, qcols), qcols)
@@ -234,8 +235,8 @@
         s_ref[...] = uk_buf[lax.rem(g, n_uk)].astype(f32).reshape(latent * grp, nope)
         for h in range(grp):
             at = h * (nope + rope)
-            turn_ref[h % 2, :nope, :latent] = s_ref[pl.ds(h, latent, stride=grp), :].astype(bf16).T
-            lat = jnp.dot(q[:, at:at + nope].astype(bf16), turn_ref[h % 2, :nope, :latent], preferred_element_type=f32)
+            p_ref[:nope, (h % 2) * latent:(h % 2 + 1) * latent] = s_ref[pl.ds(h, latent, stride=grp), :].astype(bf16).T
+            lat = jnp.dot(q[:, at:at + nope].astype(bf16), p_ref[:nope, (h % 2) * latent:(h % 2 + 1) * latent], preferred_element_type=f32)
             rows = pl.ds(pl.multiple_of((core * hp + g * grp + h) * n_req, n_req), n_req)
             for j in range(n_lat):
                 q_ref[j, rows, :] = lat[:, j * 128:(j + 1) * 128]
@@ -287,6 +288,15 @@
     def query(b):
         q = jnp.concatenate([q_ref[j, pl.ds(b, heads, stride=n_req), :].astype(bf16) for j in range(n_lat)], axis=1)
         return q, q_ref[n_lat, pl.ds(b, heads, stride=n_req), :][:, :rope].astype(bf16), ctx_ref[b] - base
+
+    def stage(b, row):
+        q, qr, _ = query(row)
+        qs_ref[lax.rem(b, 2), :, :latent] = q
+        qs_ref[lax.rem(b, 2), :, latent:] = jnp.concatenate([qr, qr], axis=1)
+
+    def staged(b):
+        slot = lax.rem(b, 2)
+        return qs_ref[slot, :, :latent], qs_ref[slot, :, latent:latent + rope], ctx_ref[b] - base
 
     def scores(b, query_b, i):
         q, qr, limit = query_b
@@ -355,6 +365,7 @@
             cp.wait()
     top = None
     query_0 = query(0)
+    stage(1, 1)
     for i in range(n_chunks):
         t = scores(0, query_0, i)
         top = t if top is None else jnp.maximum(top, t)
@@ -375,7 +386,7 @@
                 uv_copy(i).start()
 
         old = top_ref[...]
-        query_b = query(b)
+        query_b = staged(b)
         top, mass, acc = None, None, None
         for half in (0, 1):
             for cp in c_copies(b, half):
@@ -385,6 +396,9 @@
                 t = scores(b, query_b, i)
                 top = t if top is None else jnp.maximum(top, t)
                 acc = add(acc, values(r, i))
+
+            if half == 0:
+                stage(b + 1, lax.rem(b + 1, n_req))
 
             @pl.when(b + 2 < n_req)
             def _():
@@ -476,21 +490,46 @@
 
         return carry
 
-    lax.fori_loop(0, 4, first, 0)
-    to_pair(3).start()
+    lax.fori_loop(0, 3, first, 0)
+    to_pair(2).start()
 
     def second(i, carry):
-        part = block(i + 4)
+        part = block(i + 3)
         to_pair(i).wait_recv()
         sum_ref[i] = part + pair_ref[i]
 
-        @pl.when((i >= 1) & (i < 4))
+        @pl.when(i >= 1)
         def _():
             to_owner(i - 1).start()
 
         return carry
 
-    lax.fori_loop(0, 4, second, 0)
+    lax.fori_loop(0, 3, second, 0)
+
+    def third(i, carry):
+        @pl.when(i == 0)
+        def _():
+            to_owner(2).start()
+
+        @pl.when(i == 1)
+        def _():
+            to_pair(3).start()
+
+        part = block(i + 6)
+
+        @pl.when(i == 0)
+        def _():
+            po_ref[3] = part
+
+        @pl.when(i == 1)
+        def _():
+            sum_ref[3] = part
+
+        return carry
+
+    lax.fori_loop(0, 2, third, 0)
+    to_pair(3).wait_recv()
+    sum_ref[3] = sum_ref[3] + pair_ref[3]
     for i in range(3):
         to_owner(i).wait_recv()
     my_cols = pl.ds(pl.multiple_of(core * half_cols + chip * qcols, qcols), qcols)
@@ -540,7 +579,8 @@
     pl.run_scoped(
         lambda *scoped: decode_body(dims, *scoped, *refs),
         pltpu.VMEM((n_slots, t_dev, latent), jnp.bfloat16), pltpu.VMEM((n_slots, rope, t_dev), jnp.bfloat16),
-        pltpu.VMEM((heads, t_dev), jnp.bfloat16), pltpu.VMEM((2, latent, max(t_chunk, latent)), jnp.bfloat16))
+        pltpu.VMEM((heads, t_dev), jnp.bfloat16), pltpu.VMEM((2, latent, t_chunk), jnp.bfloat16),
+        pltpu.VMEM((2, heads, latent + 2 * rope), jnp.bfloat16))
 
 
 def decode(x, w_dq, g_q, w_uq, w_dkv, g_kv, w_uk, w_uv, w_o, cache_c, cache_kr, ctx_len):
@@ -551,7 +591,7 @@
     v_dim = w_uv.shape[2]
     t_dev = cache_c.shape[1]
     scale = (nope + rope) ** -0.5
-    n_dq, n_kv, n_uq, n_uk, grp, n_slots, n_split, t_chunk = 14, 7, 4, 2, 8, 3, 4, 512
+    n_dq, n_kv, n_uq, n_uk, grp, n_slots, n_split, t_chunk = 14, 7, 4, 2, 8, 3, 4, 256
     f32, bf16 = jnp.float32, jnp.bfloat16
     dims = (n_req, heads, latent, nope, rope, v_dim, low, d_model, t_dev, t_chunk, n_dq, n_kv, n_uq, n_uk, grp, n_slots, n_split, scale)
     lane = jnp.arange(rope)

time: 99.2 us -> 97.2 us (0.980)
  Pallas kernels: 94 us -> 92 us
    pallas_call x1, Pallas kernels: 94 us -> 92 us  [decode(): pl.pallas_call(functools.partial(scoped_body, dims), out_shape=jax.ShapeD...]
where the time goes in v3:
time: 97.2 us; the launch traced here: 97 us
  Pallas kernels  92 us (95%)
  other arithmetic  2.46 us (3%)
  local copies, waits for them, and re-layouts  1.9 us (2%)
    pallas_call x1, Pallas kernels, decode(): pl.pallas_call(functools.partial(scoped_body, dims), out_shape=jax.ShapeD...  92 us

profile of v3, /device:TPU:0, one launch (start us, length us, event | category | flops | bytes accessed | tf_op | source)
XLA Modules:
  0.0 97.0 jit_solution(15266319206039335308)
XLA Ops:
  0.6 0.7 convert_element_type.13
  1.3 0.7 fusion.refs_4_
  2.0 92.0 %decode.1 = f32[16,7808]{1,0:T(8,128)} custom-call(s32[16]{0:T(128)} %refs_0_.1, bf16[16,7168]{1,0:T(8,128)(2,1)} %refs_1_.1, f32[1536]{0:T(1024)} %refs_2_.1, f32[512]{0:T(512)} %refs_3_.1, f32[16,64]{1,0:T(8,128)} %fusion.refs_4_, bf16[7168,1536]{1,0:T(8,128)(2,1)} %refs_5_.1, bf16[1536,24576]{1,0:T(8,128)(2,1)} %refs_6_.1, bf16[576,7168]{1,0:T(8,128)(2,1)} %bitcast.3, ...), custom_call_target="tpu_custom_call" | custom-call | tf_op jit(solution)/shard_map/decode/pallas_call | solution.py:610
  94.1 1.1 %convert.5 = bf16[16,7808]{1,0:T(8,128)(2,1)S(1)} convert(f32[16,7808]{1,0:T(8,128)} %decode.1) | non-fusion elementwise | flops 124928 | bytes 749568 | tf_op jit(solution)/shard_map/convert.2
  95.1 0.6 slice.17
  95.7 0.6 slice.16
  96.3 0.7 slice.15
  (2 shorter events, 0.0 us)

commit v4 on v3

--- a/solution.py
+++ b/solution.py
@@ -591,7 +591,7 @@
     v_dim = w_uv.shape[2]
     t_dev = cache_c.shape[1]
     scale = (nope + rope) ** -0.5
-    n_dq, n_kv, n_uq, n_uk, grp, n_slots, n_split, t_chunk = 14, 7, 4, 2, 8, 3, 4, 256
+    n_dq, n_kv, n_uq, n_uk, grp, n_slots, n_split, t_chunk = 14, 7, 4, 2, 8, 3, 4, 512
     f32, bf16 = jnp.float32, jnp.bfloat16
     dims = (n_req, heads, latent, nope, rope, v_dim, low, d_model, t_dev, t_chunk, n_dq, n_kv, n_uq, n_uk, grp, n_slots, n_split, scale)
     lane = jnp.arange(rope)

time: 97.2 us -> 98.6 us (1.014)
  Pallas kernels: 92 us -> 93.4 us
    pallas_call x1, Pallas kernels: 92 us -> 93.4 us  [decode(): pl.pallas_call(functools.partial(scoped_body, dims), out_shape=jax.ShapeD...]
where the time goes in v4:
time: 98.6 us; the launch traced here: 98.4 us
  Pallas kernels  93.4 us (95%)
  other arithmetic  2.46 us (2%)
  local copies, waits for them, and re-layouts  1.9 us (2%)
    pallas_call x1, Pallas kernels, decode(): pl.pallas_call(functools.partial(scoped_body, dims), out_shape=jax.ShapeD...  93.4 us

profile of v4, /device:TPU:0, one launch (start us, length us, event | category | flops | bytes accessed | tf_op | source)
XLA Modules:
  0.0 98.4 jit_solution(2560046598713531767)
XLA Ops:
  0.6 0.7 convert_element_type.13
  1.3 0.7 fusion.refs_4_
  2.0 93.4 %decode.1 = f32[16,7808]{1,0:T(8,128)} custom-call(s32[16]{0:T(128)} %refs_0_.1, bf16[16,7168]{1,0:T(8,128)(2,1)} %refs_1_.1, f32[1536]{0:T(1024)} %refs_2_.1, f32[512]{0:T(512)} %refs_3_.1, f32[16,64]{1,0:T(8,128)} %fusion.refs_4_, bf16[7168,1536]{1,0:T(8,128)(2,1)} %refs_5_.1, bf16[1536,24576]{1,0:T(8,128)(2,1)} %refs_6_.1, bf16[576,7168]{1,0:T(8,128)(2,1)} %bitcast.3, ...), custom_call_target="tpu_custom_call" | custom-call | tf_op jit(solution)/shard_map/decode/pallas_call | solution.py:610
  95.5 1.1 %convert.5 = bf16[16,7808]{1,0:T(8,128)(2,1)S(1)} convert(f32[16,7808]{1,0:T(8,128)} %decode.1) | non-fusion elementwise | flops 124928 | bytes 749568 | tf_op jit(solution)/shard_map/convert.2
  96.5 0.6 slice.17
  97.1 0.6 slice.16
  97.7 0.7 slice.15
  (2 shorter events, 0.0 us)
